TPU v7x, 256 devices: a whole 4x4x8 slice. The times are simulated.
256 devices in a mesh: fft: 32 (over x_lo, z, core), scal: 8 (over x_hi, y).
Axes of the slice: x: 4 (x_hi: 2, x_lo: 2; x = x_hi * 2 + x_lo), y: 4, z: 8, core: 2. Of those that a mesh axis runs over, the one named last changes fastest.
Arguments:
- scalar_state: float32 [8, 2, 256, 256, 128], P('scal', None, 'fft'), may hold values from -12 to 12
- velocity: bfloat16 [3, 256, 256, 256], P(None, 'fft', 'scal'), may hold values from -6 to 6
- species: int32 [8], P('scal'), may hold values from 0 to 63
- kappa_table: float32 [64], replicated, may hold values from 0.1 to 1
- dealias_bound: int32 [8], P('scal'), may hold values from 64 to 85
Outputs:
- new_state: float32 [8, 2, 256, 256, 128], P('scal', None, 'fft')
- kappa: float32 [8], P('scal')
All inputs are finite; a program needn't handle non-finite values.
Results may differ from a plain program's by a relative error of at most 0.0027.
Values may be sent and summed in bfloat16 or wider, within the bound.
A program may use at most 128 MiB of HBM per device.

v0:
```python
import math
import jax
import jax.numpy as jnp
from jax import lax
from jax.sharding import PartitionSpec as P

cfl_number = 0.2


def in_one_piece(arrays, axis, split_dim, concat_dim, along):
    widths = [a.shape[along] for a in arrays]
    both = jnp.concatenate(arrays, axis=along)
    out = lax.all_to_all(both, axis, split_axis=split_dim, concat_axis=concat_dim, tiled=True)
    return tuple(jnp.split(out, [sum(widths[:k]) for k in range(1, len(widths))], axis=along))


def copy_for_each(x, axis):
    count = lax.axis_size(axis)
    return lax.all_to_all(jnp.broadcast_to(x[None], (count, *x.shape)), axis, 0, 0, tiled=True)


def collected_together(x, axis):
    leaves = jax.tree.leaves(x)
    sequence = sorted(range(len(leaves)), key=lambda k: -leaves[k].size)
    width = (1, *leaves[sequence[0]].shape)[-1]
    lines = [
        jnp.pad(leaves[k].reshape(-1), (0, -leaves[k].size % width)).reshape(-1, width)
        for k in sequence
    ]
    both, at, found = (copy_for_each(jnp.concatenate(lines), axis), 0, {})
    for k, line in zip(sequence, lines):
        section = both[:, at : at + len(line)].reshape(len(both), -1)
        found[k] = section[:, : leaves[k].size].reshape(-1, *leaves[k].shape)
        at += len(line)
    numbers = iter(range(len(leaves)))
    return jax.tree.map(lambda _: found[next(numbers)], x)


def folded_in_pairs(pieces, combine):
    while len(jax.tree.leaves(pieces)[0]) > 1:
        pieces = jax.vmap(combine)(
            *(jax.tree.map(lambda part: part[side::2], pieces) for side in (0, 1))
        )
    return jax.tree.map(lambda part: part[0], pieces)


def combined_all(x, axis, combine):
    pieces = collected_together(x, axis)
    return folded_in_pairs(pieces, combine)


def twiddle(size_in, size_out, length):
    row_index = jnp.arange(size_in, dtype=jnp.int32)[:, None]
    col_index = jnp.arange(size_out, dtype=jnp.int32)[None, :]
    angles = (row_index * col_index % length).astype(jnp.float32) * (2.0 * math.pi / length)
    norming = 1.0 / math.sqrt(length)
    return (jnp.cos(angles) * norming, jnp.sin(angles) * norming)


def build_tables(length):
    half_len = length // 2
    full_cos, full_sin = twiddle(length, length, length)
    inv_cos, inv_sin = twiddle(half_len, length, length)
    weight = jnp.where(jnp.arange(half_len, dtype=jnp.int32) == 0, 1.0, 2.0).astype(jnp.float32)[
        :, None
    ]
    fwd_cos, fwd_sin = twiddle(length, half_len, length)
    listed = (full_cos, full_sin, inv_cos * weight, inv_sin * weight, fwd_cos, fwd_sin)
    return tuple((matrix.astype(jnp.bfloat16) for matrix in listed))


def product(formula, operand, matrix):
    return jnp.einsum(formula, operand, matrix, preferred_element_type=jnp.float32)


def complex_section(real_part, imag_part, cos_matrix, sin_matrix, formula, inverse):
    real_cos = product(formula, real_part, cos_matrix)
    real_sin = product(formula, real_part, sin_matrix)
    imag_cos = product(formula, imag_part, cos_matrix)
    imag_sin = product(formula, imag_part, sin_matrix)
    if inverse:
        return (real_cos - imag_sin, real_sin + imag_cos)
    return (real_cos + imag_sin, imag_cos - real_sin)


def combine_stats(earlier, later):
    return (earlier[0] + later[0], earlier[1] + later[1], jnp.maximum(earlier[2], later[2]))


def times_wave(wavenumber, real_part, imag_part):
    new_real = (-wavenumber * imag_part.astype(jnp.float32)).astype(jnp.bfloat16)
    new_imag = (wavenumber * real_part.astype(jnp.float32)).astype(jnp.bfloat16)
    return (new_real, new_imag)


def body(scalar_state, velocity, species, kappa_table, dealias_bound):
    ky_local = scalar_state.shape[2]
    length = scalar_state.shape[3]
    half_len = length // 2
    total_count = kappa_table.shape[0]
    full_cos, full_sin, inv_cos, inv_sin, fwd_cos, fwd_sin = build_tables(length)
    ky_index = lax.axis_index("fft") * ky_local + jnp.arange(ky_local, dtype=jnp.int32)
    ky_wave = jnp.where(ky_index < half_len, ky_index, ky_index - length).astype(jnp.float32)[
        :, None, None
    ]
    kz_index = jnp.arange(length, dtype=jnp.int32)
    signed_full = jnp.where(kz_index < half_len, kz_index, kz_index - length).astype(jnp.float32)
    kz_wave = signed_full[None, :, None]
    ky_whole = signed_full[:, None, None]
    kx_wave = jnp.arange(half_len, dtype=jnp.int32).astype(jnp.float32)[None, None, :]
    ksquare = kx_wave * kx_wave + ky_wave * ky_wave + kz_wave * kz_wave
    weight = jnp.where(kx_wave == 0.0, 1.0, 2.0).astype(jnp.float32)
    cell_count = float(length) ** 3
    step_size = cfl_number * 2.0 * math.pi / length
    speeds = lax.all_gather(velocity, "scal", axis=2, tiled=True)

    def finish_inverse(halves):
        y_section = complex_section(
            halves[0], halves[1], full_cos, full_sin, "...yzx,yw->...zwx", True
        )
        y_real = y_section[0].astype(jnp.bfloat16)
        y_imag = y_section[1].astype(jnp.bfloat16)
        return product("...zwk,kx->...zwx", y_real, inv_cos) - product(
            "...zwk,kx->...zwx", y_imag, inv_sin
        )

    def gradient_set(real_part, imag_part):
        pair_real = jnp.stack([real_part, -kz_wave * imag_part]).astype(jnp.bfloat16)
        pair_imag = jnp.stack([imag_part, kz_wave * real_part]).astype(jnp.bfloat16)
        z_section = complex_section(
            pair_real, pair_imag, full_cos, full_sin, "...ykx,kz->...yzx", True
        )
        z_real = z_section[0].astype(jnp.bfloat16)
        z_imag = z_section[1].astype(jnp.bfloat16)
        came_real, came_imag = in_one_piece((z_real, z_imag), "fft", 2, 1, 0)
        x_real, x_imag = times_wave(kx_wave, came_real[0], came_imag[0])
        y_real, y_imag = times_wave(ky_whole, came_real[0], came_imag[0])
        all_real = jnp.stack([x_real, y_real, came_real[1]])
        all_imag = jnp.stack([x_imag, y_imag, came_imag[1]])
        return finish_inverse((all_real, all_imag))

    def advect(gradients):
        total = speeds[0].astype(jnp.float32) * gradients[0]
        total = total + speeds[1].astype(jnp.float32) * gradients[1]
        total = total + speeds[2].astype(jnp.float32) * gradients[2]
        return total.astype(jnp.bfloat16)

    def finish_forward(halves):
        return complex_section(halves[0], halves[1], full_cos, full_sin, "...wzk,zv->...wvk", False)

    def tendency(advected, bound):
        real_x = product("zyx,xk->zyk", advected, fwd_cos).astype(jnp.bfloat16)
        imag_x = (-product("zyx,xk->zyk", advected, fwd_sin)).astype(jnp.bfloat16)
        y_section = complex_section(real_x, imag_x, full_cos, full_sin, "zyk,yw->wzk", False)
        y_real = y_section[0].astype(jnp.bfloat16)
        y_imag = y_section[1].astype(jnp.bfloat16)
        spectral = finish_forward(
            (
                lax.all_to_all(y_real, "fft", split_axis=0, concat_axis=1, tiled=True),
                lax.all_to_all(y_imag, "fft", split_axis=0, concat_axis=1, tiled=True),
            )
        )
        dealias_mask = (ksquare <= bound * bound).astype(jnp.float32)
        return (-dealias_mask * spectral[0], -dealias_mask * spectral[1])

    scalar = 0
    start_real = scalar_state[scalar, 0]
    start_imag = scalar_state[scalar, 1]
    energy = start_real * start_real + start_imag * start_imag
    local_var = [jnp.sum(weight * energy) / cell_count]
    local_grad = [jnp.sum(weight * ksquare * energy) / cell_count]
    gradients = gradient_set(start_real, start_imag)
    magnitude = jnp.sqrt(
        gradients[0] * gradients[0] + gradients[1] * gradients[1] + gradients[2] * gradients[2]
    )
    local_peak = [jnp.max(magnitude)]
    advect_saved = [advect(gradients)]
    var_part = jnp.stack(local_var)
    grad_part = jnp.stack(local_grad)
    peak_part = jnp.stack(local_peak)
    variance, mean_grad, peak_value = combined_all(
        (var_part, grad_part, peak_part), "fft", combine_stats
    )
    matches = species[:, None] == jnp.arange(total_count, dtype=jnp.int32)[None, :]
    base_kappa = jnp.sum(jnp.where(matches, kappa_table[None, :], 0.0), axis=1)
    kappa = base_kappa * peak_value * jnp.sqrt(variance) / (mean_grad + 1e-06)
    scalar = 0
    start_real = scalar_state[scalar, 0]
    start_imag = scalar_state[scalar, 1]
    factor = jnp.exp(-kappa[scalar] * ksquare * step_size)
    bound = dealias_bound[scalar].astype(jnp.float32)
    first_real, first_imag = tendency(advect_saved[scalar], bound)
    mid_real = factor * (start_real + step_size * first_real)
    mid_imag = factor * (start_imag + step_size * first_imag)
    second_real, second_imag = tendency(advect(gradient_set(mid_real, mid_imag)), bound)
    new_real = factor * start_real + 0.5 * step_size * (factor * first_real + second_real)
    new_imag = factor * start_imag + 0.5 * step_size * (factor * first_imag + second_imag)
    updated_list = [jnp.stack([new_real, new_imag])]
    return (jnp.stack(updated_list), kappa)


def solution(mesh):
    placed = (
        P("scal", None, "fft", None, None),
        P(None, "fft", "scal", None),
        P("scal"),
        P(),
        P("scal"),
    )
    return jax.shard_map(
        body,
        mesh=mesh,
        in_specs=placed,
        out_specs=(P("scal", None, "fft", None, None), P("scal")),
        check_vma=False,
    )
```

profile of v0, /device:TPU:1, one launch (start us, length us, event | category | flops | bytes accessed | tf_op | source)
XLA Modules:
  0.0 341.0 jit_solution(12632958124329488233)
XLA Ops:
  7.2 1.9 bitcast_convert_fusion
  9.7 1.4 fusion.55
  11.1 1.3 fusion.56
  12.4 1.4 fusion.13
  13.8 1.4 fusion.12
  15.3 2.7 copy.71
  18.0 11.1 %all-to-all-start = ((bf16[4,8,256,128]{3,1,0,2:T(8,128)(2,1)}), bf16[4,8,256,128]{3,1,0,2:T(8,128)(2,1)}, u32[]{:S(2)}, u32[]{:S(2)}) async-start(bf16[4,8,256,128]{3,1,0,2:T(8,128)(2,1)} %copy.71), calls=%async_computation | async-start | bytes 4194304 | tf_op jit(solution)/shard_map/all_to_all | solution.py:13
  29.9 0.9 multiply_reduce_fusion
  32.1 46.3 %all-to-all-done = bf16[4,8,256,128]{3,1,0,2:T(8,128)(2,1)} async-done(((bf16[4,8,256,128]{3,1,0,2:T(8,128)(2,1)}), bf16[4,8,256,128]{3,1,0,2:T(8,128)(2,1)}, u32[]{:S(2)}, u32[]{:S(2)}) %all-to-all-start) | async-done | bytes 2097184 | tf_op jit(solution)/shard_map/all_to_all | solution.py:13
  78.4 2.4 copy.150
  82.1 3.1 fusion.60
  85.2 3.1 fusion.59
  88.3 1.1 multiply_convert_fusion.7
  89.4 7.1 %fusion.10 = f32[3,8,256,256]{3,2,1,0:T(8,128)} fusion(f32[256,3,8,128]{3,0,2,1:T(8,128)} %fusion.60, bf16[1,256,8,128]{3,1,2,0:T(8,128)(2,1)S(1)} %copy.82, bf16[1,256,8,128]{3,1,2,0:T(8,128)(2,1)} %get-tuple-element.32, bf16[1,256,8,128]{3,1,2,0:T(8,128)(2,1)S(1)} %get-tuple-element.31, f32[128]{0:T(128)S(1)} %fusion.155), kind=kOutput, calls=%fused_computation.39 | convolution fusion | flops 813170688 | bytes 11010560 | tf_op jit(solution)/shard_map/...zwk,kx->...zwx/dot_general | solution.py:73
  96.5 9.0 %convolution_subtract_fusion.1 = f32[3,8,256,256]{3,2,1,0:T(8,128)} fusion(f32[3,8,256,256]{3,2,1,0:T(8,128)} %fusion.10, f32[256,3,8,128]{3,0,2,1:T(8,128)} %fusion.59, bf16[1,256,8,128]{3,1,2,0:T(8,128)(2,1)S(1)} %copy.82, bf16[1,256,8,128]{3,1,2,0:T(8,128)(2,1)} %get-tuple-element.32, bf16[1,256,8,128]{3,1,2,0:T(8,128)(2,1)S(1)} %get-tuple-element.31, ...), kind=kOutput, calls=%fused_computation.5 | convolution fusion | flops 814743552 | bytes 17302016 | tf_op jit(solution)/shard_map/...zwk,kx->...zwx/dot_general | solution.py:73
  105.5 5.7 %sqrt_reduce_fusion = (f32[]{:T(128)}, bf16[8,256,256]{2,1,0:T(8,128)(2,1)S(1)}) fusion(f32[3,8,256,256]{3,2,1,0:T(8,128)} %convolution_subtract_fusion.1, bf16[3,8,256,256]{3,2,1,0:T(8,128)(2,1)} %all-gather.2.cloned.1.call-done), kind=kLoop, calls=%fused_computation.23 | loop fusion | flops 7864319 | bytes 10485764 | tf_op jit(solution)/shard_map/reduce_max | solution.py:176
  111.3 1.4 fusion.32
  112.7 1.7 convolution_convert_fusion.1
  114.4 1.2 fusion.110
  116.9 6.6 %all-to-all-start.1 = ((f32[32,3,1]{1,2,0:T(1,128)}), f32[32,3,1]{1,2,0:T(1,128)S(1)}, u32[]{:S(2)}, u32[]{:S(2)}) async-start(f32[32,3,1]{1,2,0:T(1,128)} %broadcast_in_dim.23), calls=%async_computation.1 | async-start | bytes 32768 | tf_op jit(solution)/shard_map/all_to_all | solution.py:19
  123.5 2.2 fusion.35
  125.8 1.1 copy.85
  126.9 4.5 %all-to-all-done.1 = f32[32,3,1]{1,2,0:T(1,128)S(1)} async-done(((f32[32,3,1]{1,2,0:T(1,128)}), f32[32,3,1]{1,2,0:T(1,128)S(1)}, u32[]{:S(2)}, u32[]{:S(2)}) %all-to-all-start.1) | async-done | bytes 416 | tf_op jit(solution)/shard_map/all_to_all | solution.py:19
  131.4 4.3 %all-to-all-start.3 = ((bf16[256,8,128]{2,1,0:T(8,128)(2,1)}), bf16[256,8,128]{2,1,0:T(8,128)(2,1)S(1)}, u32[]{:S(2)}, u32[]{:S(2)}) async-start(bf16[256,8,128]{2,1,0:T(8,128)(2,1)} %copy.85), calls=%async_computation.3 | async-start | bytes 1048576 | tf_op jit(solution)/shard_map/all_to_all | solution.py:160
  135.8 2.2 fusion.113
  138.0 1.2 fusion.34
  139.2 1.1 copy.83
  140.4 12.1 %all-to-all-done.3 = bf16[256,8,128]{2,1,0:T(8,128)(2,1)S(1)} async-done(((bf16[256,8,128]{2,1,0:T(8,128)(2,1)}), bf16[256,8,128]{2,1,0:T(8,128)(2,1)S(1)}, u32[]{:S(2)}, u32[]{:S(2)}) %all-to-all-start.3) | async-done | bytes 524320 | tf_op jit(solution)/shard_map/all_to_all | solution.py:160
  152.5 5.8 %all-to-all-start.2 = ((bf16[256,8,128]{2,1,0:T(8,128)(2,1)}), bf16[256,8,128]{2,1,0:T(8,128)(2,1)S(1)}, u32[]{:S(2)}, u32[]{:S(2)}) async-start(bf16[256,8,128]{2,1,0:T(8,128)(2,1)} %copy.83), calls=%async_computation.2 | async-start | bytes 1048576 | tf_op jit(solution)/shard_map/all_to_all | solution.py:159
  160.2 0.9 slice_reduce_fusion
  169.8 2.2 fusion.72
  172.0 2.8 all-to-all-done.2
  174.8 1.2 fusion.70
  176.0 2.5 fusion.29
  178.5 1.2 fusion.31
  180.7 1.3 fusion.53
  182.0 1.3 fusion.54
  183.4 1.4 fusion.15
  184.8 1.4 fusion.14
  186.5 1.4 copy.87
  187.9 54.4 %all_to_all.107 = bf16[4,8,256,128]{3,1,0,2:T(8,128)(2,1)S(1)} all-to-all(bf16[4,8,256,128]{3,1,0,2:T(8,128)(2,1)S(1)} %copy.87), channel_id=1, replica_groups=mesh['fft'=32,'scal'=8] {'fft'}, dimensions={2} | all-to-all | bytes 4194304 | tf_op jit(solution)/shard_map/all_to_all | solution.py:13
  244.0 3.1 fusion.58
  247.1 3.1 fusion.57
  250.6 1.1 multiply_convert_fusion.1
  251.7 7.1 %fusion.7 = f32[3,8,256,256]{3,2,1,0:T(8,128)} fusion(f32[256,3,8,128]{3,0,2,1:T(8,128)} %fusion.58, bf16[1,256,8,128]{3,1,2,0:T(8,128)(2,1)S(1)} %copy.98, bf16[1,256,8,128]{3,1,2,0:T(8,128)(2,1)} %get-tuple-element.28, bf16[1,256,8,128]{3,1,2,0:T(8,128)(2,1)S(1)} %get-tuple-element.27, f32[128]{0:T(128)S(1)} %fusion.155), kind=kOutput, calls=%fused_computation.36 | convolution fusion | flops 813170688 | bytes 11010560 | tf_op jit(solution)/shard_map/...zwk,kx->...zwx/dot_general | solution.py:73
  258.8 8.9 %convolution_subtract_fusion = f32[3,8,256,256]{3,2,1,0:T(8,128)} fusion(f32[3,8,256,256]{3,2,1,0:T(8,128)} %fusion.7, f32[256,3,8,128]{3,0,2,1:T(8,128)} %fusion.57, bf16[1,256,8,128]{3,1,2,0:T(8,128)(2,1)S(1)} %copy.98, bf16[1,256,8,128]{3,1,2,0:T(8,128)(2,1)} %get-tuple-element.28, bf16[1,256,8,128]{3,1,2,0:T(8,128)(2,1)S(1)} %get-tuple-element.27, ...), kind=kOutput, calls=%fused_computation.4 | convolution fusion | flops 814743552 | bytes 17302016 | tf_op jit(solution)/shard_map/...zwk,kx->...zwx/dot_general | solution.py:73
  267.7 4.5 %fusion.48 = bf16[8,256,256]{2,1,0:T(8,128)(2,1)S(1)} fusion(f32[3,8,256,256]{3,2,1,0:T(8,128)} %convolution_subtract_fusion, bf16[3,8,256,256]{3,2,1,0:T(8,128)(2,1)} %all-gather.2.cloned.1.call-done), kind=kLoop, calls=%fused_computation.89 | loop fusion | flops 4718592 | bytes 10485760 | tf_op jit(solution)/shard_map/add | solution.py:145
  272.2 0.9 fusion.33
  273.1 1.3 convolution_convert_fusion
  274.4 1.2 fusion.104
  275.6 1.2 fusion.37
  276.9 1.1 copy.101
  278.0 5.9 %all-to-all-start.6 = ((bf16[256,8,128]{2,1,0:T(8,128)(2,1)}), bf16[256,8,128]{2,1,0:T(8,128)(2,1)S(1)}, u32[]{:S(2)}, u32[]{:S(2)}) async-start(bf16[256,8,128]{2,1,0:T(8,128)(2,1)} %copy.101), calls=%async_computation.6 | async-start | bytes 1048576 | tf_op jit(solution)/shard_map/all_to_all | solution.py:160
  283.9 2.2 fusion.107
  286.1 1.2 fusion.36
  287.4 1.2 copy.99
  288.5 12.0 %all-to-all-done.6 = bf16[256,8,128]{2,1,0:T(8,128)(2,1)S(1)} async-done(((bf16[256,8,128]{2,1,0:T(8,128)(2,1)}), bf16[256,8,128]{2,1,0:T(8,128)(2,1)S(1)}, u32[]{:S(2)}, u32[]{:S(2)}) %all-to-all-start.6) | async-done | bytes 524320 | tf_op jit(solution)/shard_map/all_to_all | solution.py:160
  301.3 6.6 %all-to-all-start.5 = ((bf16[256,8,128]{2,1,0:T(8,128)(2,1)}), bf16[256,8,128]{2,1,0:T(8,128)(2,1)}, u32[]{:S(2)}, u32[]{:S(2)}) async-start(bf16[256,8,128]{2,1,0:T(8,128)(2,1)} %copy.99), calls=%async_computation.5 | async-start | bytes 1048576 | tf_op jit(solution)/shard_map/all_to_all | solution.py:159
  307.9 3.3 fusion.66
  311.2 13.2 %all-to-all-done.5 = bf16[256,8,128]{2,1,0:T(8,128)(2,1)} async-done(((bf16[256,8,128]{2,1,0:T(8,128)(2,1)}), bf16[256,8,128]{2,1,0:T(8,128)(2,1)}, u32[]{:S(2)}, u32[]{:S(2)}) %all-to-all-start.5) | async-done | bytes 524320 | tf_op jit(solution)/shard_map/all_to_all | solution.py:159
  324.5 2.2 fusion.64
  326.7 3.0 fusion.21
  329.8 1.5 fusion.27
  331.4 1.5 maximum_bitcast_fusion
  (98 shorter events, 13.2 us)
Async XLA Ops:
  7.2 2.2 copy-start
  18.0 60.4 %all-to-all-start = ((bf16[4,8,256,128]{3,1,0,2:T(8,128)(2,1)}), bf16[4,8,256,128]{3,1,0,2:T(8,128)(2,1)}, u32[]{:S(2)}, u32[]{:S(2)}) async-start(bf16[4,8,256,128]{3,1,0,2:T(8,128)(2,1)} %copy.71), calls=%async_computation | async-start | bytes 4194304 | tf_op jit(solution)/shard_map/all_to_all | solution.py:13
  29.1 76.4 %all-gather.2.cloned.1.call-start = ((), (), s32[]{:S(2)}) async-start(), calls=%async_computation.7 | async-start | bytes 3538944 | tf_op jit(solution)/shard_map/all_gather | solution.py:115
  112.7 1.7 copy-start.7
  116.9 14.5 %all-to-all-start.1 = ((f32[32,3,1]{1,2,0:T(1,128)}), f32[32,3,1]{1,2,0:T(1,128)S(1)}, u32[]{:S(2)}, u32[]{:S(2)}) async-start(f32[32,3,1]{1,2,0:T(1,128)} %broadcast_in_dim.23), calls=%async_computation.1 | async-start | bytes 32768 | tf_op jit(solution)/shard_map/all_to_all | solution.py:19
  125.8 12.2 %copy-start.8 = (bf16[8,256,128]{2,1,0:T(8,128)(2,1)S(1)}, bf16[8,256,128]{2,1,0:T(8,128)(2,1)}, u32[]{:S(2)}) copy-start(bf16[8,256,128]{2,1,0:T(8,128)(2,1)} %copy-done.7) | copy-start | bytes 1572868
  131.4 21.0 %all-to-all-start.3 = ((bf16[256,8,128]{2,1,0:T(8,128)(2,1)}), bf16[256,8,128]{2,1,0:T(8,128)(2,1)S(1)}, u32[]{:S(2)}, u32[]{:S(2)}) async-start(bf16[256,8,128]{2,1,0:T(8,128)(2,1)} %copy.85), calls=%async_computation.3 | async-start | bytes 1048576 | tf_op jit(solution)/shard_map/all_to_all | solution.py:160
  138.0 21.5 %copy-start.10 = (f32[64]{0:T(128)S(1)}, f32[64]{0:T(128)}, u32[]{:S(2)}) copy-start(f32[64]{0:T(128)} %param.8) | copy-start | bytes 772
  152.5 22.3 %all-to-all-start.2 = ((bf16[256,8,128]{2,1,0:T(8,128)(2,1)}), bf16[256,8,128]{2,1,0:T(8,128)(2,1)S(1)}, u32[]{:S(2)}, u32[]{:S(2)}) async-start(bf16[256,8,128]{2,1,0:T(8,128)(2,1)} %copy.83), calls=%async_computation.2 | async-start | bytes 1048576 | tf_op jit(solution)/shard_map/all_to_all | solution.py:159
  178.5 2.1 copy-start.3
  179.7 1.0 copy-start.1
  274.4 2.4 copy-start.9
  278.0 22.5 %all-to-all-start.6 = ((bf16[256,8,128]{2,1,0:T(8,128)(2,1)}), bf16[256,8,128]{2,1,0:T(8,128)(2,1)S(1)}, u32[]{:S(2)}, u32[]{:S(2)}) async-start(bf16[256,8,128]{2,1,0:T(8,128)(2,1)} %copy.101), calls=%async_computation.6 | async-start | bytes 1048576 | tf_op jit(solution)/shard_map/all_to_all | solution.py:160
  300.5 0.8 copy-start.5
  301.3 23.2 %all-to-all-start.5 = ((bf16[256,8,128]{2,1,0:T(8,128)(2,1)}), bf16[256,8,128]{2,1,0:T(8,128)(2,1)}, u32[]{:S(2)}, u32[]{:S(2)}) async-start(bf16[256,8,128]{2,1,0:T(8,128)(2,1)} %copy.99), calls=%async_computation.5 | async-start | bytes 1048576 | tf_op jit(solution)/shard_map/all_to_all | solution.py:159
  307.9 18.8 %copy-start.4 = (f32[8,256,128]{2,1,0:T(8,128)S(1)}, f32[8,256,128]{2,1,0:T(8,128)}, u32[]{:S(2)}) copy-start(f32[8,256,128]{2,1,0:T(8,128)} %copy-done.3) | copy-start | bytes 3145732
  326.7 3.1 copy-start.2
  326.7 3.1 copy-start.6
Sparse Core Ops, SparseCore 0:
  32.5 72.3 all-gather.1
where the time goes:
time: 348 us; the launch traced here: 341 us
  waiting for transfers between devices  91.2 us (26%)
  matrix products  90.6 us (26%)
  blocking collectives  54.4 us (16%)
  starting transfers between devices  40.6 us (12%)
  between operations  23 us (7%)
  local copies, waits for them, and re-layouts  21.8 us (6%)
  other arithmetic  19.3 us (6%)
    dot_general x36, matrix products, product(): jnp.einsum(formula, operand, matrix, preferred_element_type=jnp.float32)  90.6 us
    all_to_all x1, blocking collectives, in_one_piece(): lax.all_to_all(both, axis, split_axis=split_dim, concat_axis=concat_dim,...  54.4 us
    all_to_all x1, waiting for transfers between devices, in_one_piece(): lax.all_to_all(both, axis, split_axis=split_dim, concat_axis=concat_dim,...  46.3 us
    all_to_all x2, waiting for transfers between devices, tendency(): lax.all_to_all(y_imag, 'fft', split_axis=0, concat_axis=1, tiled=True)  24.1 us
    all_to_all x2, waiting for transfers between devices, tendency(): lax.all_to_all(y_real, 'fft', split_axis=0, concat_axis=1, tiled=True)  16 us
    all_to_all x2, starting transfers between devices, tendency(): lax.all_to_all(y_real, 'fft', split_axis=0, concat_axis=1, tiled=True)  12.4 us
    all_to_all x1, starting transfers between devices, in_one_piece(): lax.all_to_all(both, axis, split_axis=split_dim, concat_axis=concat_dim,...  11.1 us
    all_to_all x2, starting transfers between devices, tendency(): lax.all_to_all(y_imag, 'fft', split_axis=0, concat_axis=1, tiled=True)  10.2 us
  transfers between devices with their start and end apart: 7, of which 6 were waited for; matrix products, arithmetic and copies ran while one was open for 15% of the time, Pallas kernels for 0%

commit v1 on v0

--- a/solution.py
+++ b/solution.py
@@ -157,7 +157,12 @@
         spectral = finish_forward(
             (
                 lax.all_to_all(y_real, "fft", split_axis=0, concat_axis=1, tiled=True),
-                lax.all_to_all(y_imag, "fft", split_axis=0, concat_axis=1, tiled=True),
+                jnp.concatenate(
+                    lax.all_to_all(
+                        jnp.stack(jnp.split(y_imag, lax.axis_size("fft"), axis=0)), "fft", 0, 0
+                    ),
+                    axis=1,
+                ),
             )
         )
         dealias_mask = (ksquare <= bound * bound).astype(jnp.float32)

time: 348 us -> 386 us (1.11)
  local copies, waits for them, and re-layouts: 21.8 us -> 58.7 us
    unnamed x22 -> x82, local copies, waits for them, and re-layouts: 1.24 us -> 39.1 us
  transfers between devices with their start and end apart: 7 -> 7, of which waited for: 6 -> 6; matrix products, arithmetic and copies ran while one was open for 15% -> 13% of each run, Pallas kernels for 0% -> 0%
where the time goes in v1:
time: 386 us; the launch traced here: 379 us
  waiting for transfers between devices  93.7 us (24%)
  matrix products  89 us (23%)
  local copies, waits for them, and re-layouts  58.7 us (15%)
  blocking collectives  54.5 us (14%)
  starting transfers between devices  40.6 us (11%)
  between operations  23.2 us (6%)
  other arithmetic  19.1 us (5%)
    dot_general x36, matrix products, product(): jnp.einsum(formula, operand, matrix, preferred_element_type=jnp.float32)  89 us
    all_to_all x1, blocking collectives, in_one_piece(): lax.all_to_all(both, axis, split_axis=split_dim, concat_axis=concat_dim,...  54.5 us
    all_to_all x1, waiting for transfers between devices, in_one_piece(): lax.all_to_all(both, axis, split_axis=split_dim, concat_axis=concat_dim,...  46.1 us
    unnamed x82, local copies, waits for them, and re-layouts  39.1 us
    all_to_all x2, waiting for transfers between devices, tendency(): lax.all_to_all(jnp.stack(jnp.split(y_imag, lax.axis_size('fft'), axis=0))...  24.1 us
    all_to_all x2, waiting for transfers between devices, tendency(): lax.all_to_all(y_real, 'fft', split_axis=0, concat_axis=1, tiled=True)  15.9 us
    all_to_all x2, starting transfers between devices, tendency(): lax.all_to_all(y_real, 'fft', split_axis=0, concat_axis=1, tiled=True)  12.4 us
    all_to_all x1, starting transfers between devices, in_one_piece(): lax.all_to_all(both, axis, split_axis=split_dim, concat_axis=concat_dim,...  11.1 us
  transfers between devices with their start and end apart: 7, of which 6 were waited for; matrix products, arithmetic and copies ran while one was open for 13% of the time, Pallas kernels for 0%

profile of v1, /device:TPU:1, one launch (start us, length us, event | category | flops | bytes accessed | tf_op | source)
XLA Modules:
  0.0 378.9 jit_solution(11076963881745123262)
XLA Ops:
  7.2 1.9 bitcast_convert_fusion
  9.7 1.4 fusion.55
  11.1 1.3 fusion.56
  12.4 1.4 fusion.13
  13.8 1.4 fusion.12
  15.3 2.7 copy.75
  18.0 11.1 %all-to-all-start = ((bf16[4,8,256,128]{3,1,0,2:T(8,128)(2,1)}), bf16[4,8,256,128]{3,1,0,2:T(8,128)(2,1)}, u32[]{:S(2)}, u32[]{:S(2)}) async-start(bf16[4,8,256,128]{3,1,0,2:T(8,128)(2,1)} %copy.75), calls=%async_computation | async-start | bytes 4194304 | tf_op jit(solution)/shard_map/all_to_all | solution.py:13
  29.9 1.0 multiply_reduce_fusion
  32.3 46.1 %all-to-all-done = bf16[4,8,256,128]{3,1,0,2:T(8,128)(2,1)} async-done(((bf16[4,8,256,128]{3,1,0,2:T(8,128)(2,1)}), bf16[4,8,256,128]{3,1,0,2:T(8,128)(2,1)}, u32[]{:S(2)}, u32[]{:S(2)}) %all-to-all-start) | async-done | bytes 2097184 | tf_op jit(solution)/shard_map/all_to_all | solution.py:13
  78.4 2.4 copy.146
  82.1 3.1 fusion.60
  85.2 3.1 fusion.59
  88.3 1.1 multiply_convert_fusion.7
  89.5 7.1 %fusion.10 = f32[3,8,256,256]{3,2,1,0:T(8,128)} fusion(f32[256,3,8,128]{3,0,2,1:T(8,128)} %fusion.60, bf16[1,256,8,128]{3,1,2,0:T(8,128)(2,1)S(1)} %copy.86, bf16[1,256,8,128]{3,1,2,0:T(8,128)(2,1)} %get-tuple-element.32, bf16[1,256,8,128]{3,1,2,0:T(8,128)(2,1)S(1)} %get-tuple-element.31, f32[128]{0:T(128)S(1)} %fusion.151), kind=kOutput, calls=%fused_computation.39 | convolution fusion | flops 813170688 | bytes 11010560 | tf_op jit(solution)/shard_map/...zwk,kx->...zwx/dot_general | solution.py:73
  96.5 9.0 %convolution_subtract_fusion.1 = f32[3,8,256,256]{3,2,1,0:T(8,128)} fusion(f32[3,8,256,256]{3,2,1,0:T(8,128)} %fusion.10, f32[256,3,8,128]{3,0,2,1:T(8,128)} %fusion.59, bf16[1,256,8,128]{3,1,2,0:T(8,128)(2,1)S(1)} %copy.86, bf16[1,256,8,128]{3,1,2,0:T(8,128)(2,1)} %get-tuple-element.32, bf16[1,256,8,128]{3,1,2,0:T(8,128)(2,1)S(1)} %get-tuple-element.31, ...), kind=kOutput, calls=%fused_computation.5 | convolution fusion | flops 814743552 | bytes 17302016 | tf_op jit(solution)/shard_map/...zwk,kx->...zwx/dot_general | solution.py:73
  105.5 5.7 %sqrt_reduce_fusion = (f32[]{:T(128)}, bf16[8,256,256]{2,1,0:T(8,128)(2,1)S(1)}) fusion(f32[3,8,256,256]{3,2,1,0:T(8,128)} %convolution_subtract_fusion.1, bf16[3,8,256,256]{3,2,1,0:T(8,128)(2,1)} %all-gather.2.cloned.1.call-done), kind=kLoop, calls=%fused_computation.23 | loop fusion | flops 7864319 | bytes 10485764 | tf_op jit(solution)/shard_map/reduce_max | solution.py:181
  111.3 1.4 fusion.32
  112.7 0.9 convolution_convert_fusion.1
  113.6 1.2 fusion.106
  114.8 1.2 fusion.35
  136.3 6.6 %all-to-all-start.1 = ((f32[32,3,1]{1,2,0:T(1,128)}), f32[32,3,1]{1,2,0:T(1,128)S(1)}, u32[]{:S(2)}, u32[]{:S(2)}) async-start(f32[32,3,1]{1,2,0:T(1,128)} %broadcast_in_dim.23), calls=%async_computation.1 | async-start | bytes 32768 | tf_op jit(solution)/shard_map/all_to_all | solution.py:19
  143.5 7.3 %all-to-all-done.1 = f32[32,3,1]{1,2,0:T(1,128)S(1)} async-done(((f32[32,3,1]{1,2,0:T(1,128)}), f32[32,3,1]{1,2,0:T(1,128)S(1)}, u32[]{:S(2)}, u32[]{:S(2)}) %all-to-all-start.1) | async-done | bytes 416 | tf_op jit(solution)/shard_map/all_to_all | solution.py:19
  150.8 4.3 %all-to-all-start.3 = ((bf16[32,8,8,128]{3,1,2,0:T(8,128)(2,1)}), bf16[32,8,8,128]{3,1,2,0:T(8,128)(2,1)S(1)}, u32[]{:S(2)}, u32[]{:S(2)}) async-start(bf16[32,8,8,128]{3,1,2,0:T(8,128)(2,1)} %constant_dynamic-update-slice_fusion), calls=%async_computation.3 | async-start | bytes 1048576 | tf_op jit(solution)/shard_map/all_to_all | solution.py:161
  155.1 2.2 fusion.109
  157.4 1.2 fusion.34
  158.6 1.1 copy.87
  159.7 12.1 %all-to-all-done.3 = bf16[32,8,8,128]{3,1,2,0:T(8,128)(2,1)S(1)} async-done(((bf16[32,8,8,128]{3,1,2,0:T(8,128)(2,1)}), bf16[32,8,8,128]{3,1,2,0:T(8,128)(2,1)S(1)}, u32[]{:S(2)}, u32[]{:S(2)}) %all-to-all-start.3) | async-done | bytes 524320 | tf_op jit(solution)/shard_map/all_to_all | solution.py:161
  171.8 5.8 %all-to-all-start.2 = ((bf16[256,8,128]{2,1,0:T(8,128)(2,1)}), bf16[256,8,128]{2,1,0:T(8,128)(2,1)S(1)}, u32[]{:S(2)}, u32[]{:S(2)}) async-start(bf16[256,8,128]{2,1,0:T(8,128)(2,1)} %copy.87), calls=%async_computation.2 | async-start | bytes 1048576 | tf_op jit(solution)/shard_map/all_to_all | solution.py:159
  179.5 0.9 slice_reduce_fusion
  189.3 2.2 fusion.74
  191.5 2.7 all-to-all-done.2
  194.2 1.2 fusion.67
  195.4 2.5 fusion.29
  197.8 1.3 fusion.31
  199.1 0.9 convert_bitcast_fusion
  200.1 1.3 fusion.53
  201.4 1.3 fusion.54
  202.8 1.4 fusion.15
  204.1 1.6 fusion.14
  205.9 1.4 copy.91
  207.2 54.5 %all_to_all.81 = bf16[4,8,256,128]{3,1,0,2:T(8,128)(2,1)S(1)} all-to-all(bf16[4,8,256,128]{3,1,0,2:T(8,128)(2,1)S(1)} %copy.91), channel_id=1, replica_groups=mesh['fft'=32,'scal'=8] {'fft'}, dimensions={2} | all-to-all | bytes 4194304 | tf_op jit(solution)/shard_map/all_to_all | solution.py:13
  261.8 0.8 copy.145
  263.5 3.1 fusion.58
  266.6 3.1 fusion.57
  270.1 1.1 multiply_convert_fusion.1
  271.2 7.1 %fusion.7 = f32[3,8,256,256]{3,2,1,0:T(8,128)} fusion(f32[256,3,8,128]{3,0,2,1:T(8,128)} %fusion.58, bf16[1,256,8,128]{3,1,2,0:T(8,128)(2,1)S(1)} %copy.102, bf16[1,256,8,128]{3,1,2,0:T(8,128)(2,1)} %get-tuple-element.28, bf16[1,256,8,128]{3,1,2,0:T(8,128)(2,1)S(1)} %get-tuple-element.27, f32[128]{0:T(128)S(1)} %fusion.151), kind=kOutput, calls=%fused_computation.36 | convolution fusion | flops 813170688 | bytes 11010560 | tf_op jit(solution)/shard_map/...zwk,kx->...zwx/dot_general | solution.py:73
  278.3 8.9 %convolution_subtract_fusion = f32[3,8,256,256]{3,2,1,0:T(8,128)} fusion(f32[3,8,256,256]{3,2,1,0:T(8,128)} %fusion.7, f32[256,3,8,128]{3,0,2,1:T(8,128)} %fusion.57, bf16[1,256,8,128]{3,1,2,0:T(8,128)(2,1)S(1)} %copy.102, bf16[1,256,8,128]{3,1,2,0:T(8,128)(2,1)} %get-tuple-element.28, bf16[1,256,8,128]{3,1,2,0:T(8,128)(2,1)S(1)} %get-tuple-element.27, ...), kind=kOutput, calls=%fused_computation.4 | convolution fusion | flops 814743552 | bytes 17302016 | tf_op jit(solution)/shard_map/...zwk,kx->...zwx/dot_general | solution.py:73
  287.2 4.5 %fusion.48 = bf16[8,256,256]{2,1,0:T(8,128)(2,1)S(1)} fusion(f32[3,8,256,256]{3,2,1,0:T(8,128)} %convolution_subtract_fusion, bf16[3,8,256,256]{3,2,1,0:T(8,128)(2,1)} %all-gather.2.cloned.1.call-done), kind=kLoop, calls=%fused_computation.89 | loop fusion | flops 4718592 | bytes 10485760 | tf_op jit(solution)/shard_map/add | solution.py:145
  291.7 0.9 fusion.33
  292.6 1.3 convolution_convert_fusion
  293.9 1.2 fusion.100
  295.1 1.2 fusion.37
  315.9 5.9 %all-to-all-start.6 = ((bf16[32,8,8,128]{3,1,2,0:T(8,128)(2,1)}), bf16[32,8,8,128]{3,1,2,0:T(8,128)(2,1)S(1)}, u32[]{:S(2)}, u32[]{:S(2)}) async-start(bf16[32,8,8,128]{3,1,2,0:T(8,128)(2,1)} %constant_dynamic-update-slice_fusion.32), calls=%async_computation.6 | async-start | bytes 1048576 | tf_op jit(solution)/shard_map/all_to_all | solution.py:161
  321.8 2.2 fusion.103
  324.1 1.2 fusion.36
  325.3 1.2 copy.103
  326.4 12.0 %all-to-all-done.6 = bf16[32,8,8,128]{3,1,2,0:T(8,128)(2,1)S(1)} async-done(((bf16[32,8,8,128]{3,1,2,0:T(8,128)(2,1)}), bf16[32,8,8,128]{3,1,2,0:T(8,128)(2,1)S(1)}, u32[]{:S(2)}, u32[]{:S(2)}) %all-to-all-start.6) | async-done | bytes 524320 | tf_op jit(solution)/shard_map/all_to_all | solution.py:161
  339.2 6.6 %all-to-all-start.5 = ((bf16[256,8,128]{2,1,0:T(8,128)(2,1)}), bf16[256,8,128]{2,1,0:T(8,128)(2,1)}, u32[]{:S(2)}, u32[]{:S(2)}) async-start(bf16[256,8,128]{2,1,0:T(8,128)(2,1)} %copy.103), calls=%async_computation.5 | async-start | bytes 1048576 | tf_op jit(solution)/shard_map/all_to_all | solution.py:159
  345.8 3.3 fusion.69
  349.2 13.2 %all-to-all-done.5 = bf16[256,8,128]{2,1,0:T(8,128)(2,1)} async-done(((bf16[256,8,128]{2,1,0:T(8,128)(2,1)}), bf16[256,8,128]{2,1,0:T(8,128)(2,1)}, u32[]{:S(2)}, u32[]{:S(2)}) %all-to-all-start.5) | async-done | bytes 524320 | tf_op jit(solution)/shard_map/all_to_all | solution.py:159
  362.4 2.2 fusion.64
  364.7 3.0 fusion.21
  367.7 1.6 fusion.27
  369.3 1.5 maximum_bitcast_fusion
  (158 shorter events, 50.4 us)
Async XLA Ops:
  7.2 2.2 copy-start
  18.0 60.4 %all-to-all-start = ((bf16[4,8,256,128]{3,1,0,2:T(8,128)(2,1)}), bf16[4,8,256,128]{3,1,0,2:T(8,128)(2,1)}, u32[]{:S(2)}, u32[]{:S(2)}) async-start(bf16[4,8,256,128]{3,1,0,2:T(8,128)(2,1)} %copy.75), calls=%async_computation | async-start | bytes 4194304 | tf_op jit(solution)/shard_map/all_to_all | solution.py:13
  29.1 76.5 %all-gather.2.cloned.1.call-start = ((), (), s32[]{:S(2)}) async-start(), calls=%async_computation.7 | async-start | bytes 3538944 | tf_op jit(solution)/shard_map/all_gather | solution.py:115
  113.6 11.0 %copy-start.7 = (bf16[8,256,128]{2,1,0:T(8,128)(2,1)}, bf16[8,256,128]{2,1,0:T(8,128)(2,1)S(1)}, u32[]{:S(2)}) copy-start(bf16[8,256,128]{2,1,0:T(8,128)(2,1)S(1)} %convolution_convert_fusion.1) | copy-start | bytes 1572868
  136.3 14.5 %all-to-all-start.1 = ((f32[32,3,1]{1,2,0:T(1,128)}), f32[32,3,1]{1,2,0:T(1,128)S(1)}, u32[]{:S(2)}, u32[]{:S(2)}) async-start(f32[32,3,1]{1,2,0:T(1,128)} %broadcast_in_dim.23), calls=%async_computation.1 | async-start | bytes 32768 | tf_op jit(solution)/shard_map/all_to_all | solution.py:19
  150.8 21.0 %all-to-all-start.3 = ((bf16[32,8,8,128]{3,1,2,0:T(8,128)(2,1)}), bf16[32,8,8,128]{3,1,2,0:T(8,128)(2,1)S(1)}, u32[]{:S(2)}, u32[]{:S(2)}) async-start(bf16[32,8,8,128]{3,1,2,0:T(8,128)(2,1)} %constant_dynamic-update-slice_fusion), calls=%async_computation.3 | async-start | bytes 1048576 | tf_op jit(solution)/shard_map/all_to_all | solution.py:161
  157.4 21.6 %copy-start.9 = (f32[64]{0:T(128)S(1)}, f32[64]{0:T(128)}, u32[]{:S(2)}) copy-start(f32[64]{0:T(128)} %param.8) | copy-start | bytes 772
  171.8 22.3 %all-to-all-start.2 = ((bf16[256,8,128]{2,1,0:T(8,128)(2,1)}), bf16[256,8,128]{2,1,0:T(8,128)(2,1)S(1)}, u32[]{:S(2)}, u32[]{:S(2)}) async-start(bf16[256,8,128]{2,1,0:T(8,128)(2,1)} %copy.87), calls=%async_computation.2 | async-start | bytes 1048576 | tf_op jit(solution)/shard_map/all_to_all | solution.py:159
  197.8 2.2 copy-start.3
  199.1 1.0 copy-start.1
  293.9 11.0 %copy-start.8 = (bf16[8,256,128]{2,1,0:T(8,128)(2,1)}, bf16[8,256,128]{2,1,0:T(8,128)(2,1)S(1)}, u32[]{:S(2)}) copy-start(bf16[8,256,128]{2,1,0:T(8,128)(2,1)S(1)} %convolution_convert_fusion) | copy-start | bytes 1572868
  315.9 22.5 %all-to-all-start.6 = ((bf16[32,8,8,128]{3,1,2,0:T(8,128)(2,1)}), bf16[32,8,8,128]{3,1,2,0:T(8,128)(2,1)S(1)}, u32[]{:S(2)}, u32[]{:S(2)}) async-start(bf16[32,8,8,128]{3,1,2,0:T(8,128)(2,1)} %constant_dynamic-update-slice_fusion.32), calls=%async_computation.6 | async-start | bytes 1048576 | tf_op jit(solution)/shard_map/all_to_all | solution.py:161
  338.4 0.8 copy-start.5
  339.2 23.2 %all-to-all-start.5 = ((bf16[256,8,128]{2,1,0:T(8,128)(2,1)}), bf16[256,8,128]{2,1,0:T(8,128)(2,1)}, u32[]{:S(2)}, u32[]{:S(2)}) async-start(bf16[256,8,128]{2,1,0:T(8,128)(2,1)} %copy.103), calls=%async_computation.5 | async-start | bytes 1048576 | tf_op jit(solution)/shard_map/all_to_all | solution.py:159
  345.8 18.8 %copy-start.4 = (f32[8,256,128]{2,1,0:T(8,128)S(1)}, f32[8,256,128]{2,1,0:T(8,128)}, u32[]{:S(2)}) copy-start(f32[8,256,128]{2,1,0:T(8,128)} %copy-done.3) | copy-start | bytes 3145732
  364.6 3.1 copy-start.2
  364.6 3.1 copy-start.6
Sparse Core Ops, SparseCore 0:
  32.5 72.3 all-gather.1
